TPU v7x, 32 devices: a whole 2x2x4 slice. The times are simulated.
32 devices in a mesh: row: 4 (over y, core), col: 8 (over z, x).
Axes of the slice: x: 2, y: 2, z: 4, core: 2. Of those that a mesh axis runs over, the one named last changes fastest.
Arguments:
- text_features: bfloat16 [5, 1024, 3584], P(None, ('row', 'col')), may hold values from -18 to 18
- vision_features: bfloat16 [6, 1024, 1024], P(None, ('row', 'col')), may hold values from -18 to 18
Outputs:
- stimulus_terms: float32 [1024, 30], P(('row', 'col'))
- cka: float32 [5, 6], replicated
All inputs are finite; a program needn't handle non-finite values.
Results may differ from a plain program's by a relative error of at most 0.0003.
Values may be sent and summed in bfloat16 or wider, within the bound.
No kernel may reach another device: no remote copies, remote signals or barrier semaphores. Data moves between devices by JAX's collectives and lax.ppermute only.
A program may use at most 192 MiB of HBM per device.

v0:
```python
import jax
import jax.numpy as jnp
from jax import lax
from jax.sharding import PartitionSpec as P


def center_with(features, totals, stimuli_count):
    values = features.astype(jnp.float32)
    return (values - totals[:, None, :] / stimuli_count).astype(jnp.bfloat16)


def local(text_features, vision_features):
    text_layers = text_features.shape[0]
    vision_layers = vision_features.shape[0]
    stimuli_count = text_features.shape[1] * lax.axis_size("row") * lax.axis_size("col")
    text_block, vision_block = (
        lax.all_gather(text_features, "col", axis=1, tiled=True),
        lax.all_gather(vision_features, "col", axis=1, tiled=True),
    )
    text_set, vision_set = (
        lax.all_gather(text_features, "row", axis=1, tiled=True),
        lax.all_gather(vision_features, "row", axis=1, tiled=True),
    )
    text_total, vision_total = lax.psum(
        (
            jnp.sum(text_block.astype(jnp.float32), axis=1),
            jnp.sum(vision_block.astype(jnp.float32), axis=1),
        ),
        "row",
    )
    text_block = center_with(text_block, text_total, stimuli_count)
    text_set = center_with(text_set, text_total, stimuli_count)
    vision_block = center_with(vision_block, vision_total, stimuli_count)
    vision_set = center_with(vision_set, vision_total, stimuli_count)
    text_tiles = jnp.einsum(
        "lrd,lcd->lrc", text_block, text_set, preferred_element_type=jnp.float32
    )
    vision_tiles = jnp.einsum(
        "lrd,lcd->lrc", vision_block, vision_set, preferred_element_type=jnp.float32
    )
    row_share = jnp.einsum(
        "arc,brc->rab", text_tiles, vision_tiles, precision=lax.Precision.HIGHEST
    )
    block_rows = row_share.shape[0]
    cross_part = jnp.sum(row_share, axis=0)
    text_part = jnp.sum(text_tiles * text_tiles, axis=(1, 2))
    vision_part = jnp.sum(vision_tiles * vision_tiles, axis=(1, 2))
    cross, text_self, vision_self = lax.psum((cross_part, text_part, vision_part), ("row", "col"))
    own_share = lax.psum_scatter(
        row_share.reshape(block_rows, text_layers * vision_layers),
        "col",
        scatter_dimension=0,
        tiled=True,
    )
    scale = 1.0 / jnp.sqrt(text_self[:, None] * vision_self[None, :])
    stimulus_terms = own_share * (scale.reshape(1, text_layers * vision_layers) * stimuli_count)
    return (stimulus_terms, cross * scale)


def solution(mesh):
    in_specs = (P(None, ("row", "col"), None), P(None, ("row", "col"), None))
    out_specs = (P(("row", "col"), None), P())
    return jax.shard_map(local, mesh=mesh, in_specs=in_specs, out_specs=out_specs, check_vma=False)
```

profile of v0, /device:TPU:0, one launch (start us, length us, event | category | flops | bytes accessed | tf_op | source)
XLA Modules:
  0.0 381.2 jit_solution(2243413906863889780)
XLA Ops:
  7.2 0.0 all-gather.5.cloned.1.call-start
  7.2 0.7 all-gather.5.cloned.1.call-update
  7.9 0.0 all-gather.9.cloned.1.call-start
  7.9 0.7 all-gather.9.cloned.1.call-update
  8.6 0.0 all-gather.11.cloned.1.call-start
  8.7 0.7 all-gather.11.cloned.1.call-update
  9.4 0.0 all-reduce.3.cloned.1.call-start
  9.4 137.5 %all-gather.5.cloned.1.call-done = bf16[5,256,3584]{2,1,0:T(8,128)(2,1)} async-done(((bf16[5,32,3584]{2,1,0:T(8,128)(2,1)}), bf16[5,256,3584]{2,1,0:T(8,128)(2,1)}) %all-gather.5.cloned.1.call-update) | async-done | bytes 9175056 | tf_op jit(solution)/shard_map/all_gather | solution.py:17
  147.0 5.5 %convert_reduce_fusion = f32[5,3584]{1,0:T(8,128)} fusion(bf16[5,256,3584]{2,1,0:T(8,128)(2,1)} %all-gather.5.cloned.1.call-done), kind=kLoop, calls=%fused_computation.1 | loop fusion | flops 9157120 | bytes 9246720 | tf_op jit(solution)/shard_map/reduce_sum | solution.py:26
  152.5 0.0 all-reduce.3.cloned.1.call-update
  152.5 0.0 all-gather.7.cloned.1.call-start
  152.6 0.5 all-gather.7.cloned.1.call-update
  153.1 0.0 reduce-scatter.4.cloned.1.call-start
  153.2 54.2 %all-gather.9.cloned.1.call-done = bf16[6,256,1024]{2,1,0:T(8,128)(2,1)} async-done(((bf16[6,32,1024]{2,1,0:T(8,128)(2,1)}), bf16[6,256,1024]{2,1,0:T(8,128)(2,1)}) %all-gather.9.cloned.1.call-update) | async-done | bytes 3145744 | tf_op jit(solution)/shard_map/all_gather | solution.py:18
  207.4 2.5 convert_reduce_fusion.1
  209.9 11.1 %psum.36 = f32[6,1024]{1,0:T(8,128)S(1)} all-reduce(f32[6,1024]{1,0:T(8,128)S(1)} %convert_reduce_fusion.1), channel_id=1, replica_groups=mesh['row'=4,'col'=8] {'row'}, use_global_device_ids=true, to_apply=%region_3.0 | all-reduce | flops 6144 | bytes 49152 | tf_op jit(solution)/shard_map/psum | solution.py:24
  221.0 6.5 %all-gather.11.cloned.1.call-done = bf16[6,128,1024]{2,1,0:T(8,128)(2,1)} async-done(((bf16[6,32,1024]{2,1,0:T(8,128)(2,1)}), bf16[6,128,1024]{2,1,0:T(8,128)(2,1)}) %all-gather.11.cloned.1.call-update) | async-done | bytes 1572880 | tf_op jit(solution)/shard_map/all_gather | solution.py:22
  227.5 3.5 multiply_reduce_fusion
  231.0 28.9 %all-reduce.3.cloned.1.call-done = f32[5,3584]{1,0:T(8,128)} async-done(((f32[5,3584]{1,0:T(8,128)}), f32[5,3584]{1,0:T(8,128)}) %all-reduce.3.cloned.1.call-update) | async-done | bytes 71696 | tf_op jit(solution)/shard_map/psum | solution.py:24
  259.9 0.9 broadcast_multiply_fusion
  260.8 38.6 %all-gather.7.cloned.1.call-done = bf16[5,128,3584]{2,1,0:T(8,128)(2,1)} async-done(((bf16[5,32,3584]{2,1,0:T(8,128)(2,1)}), bf16[5,128,3584]{2,1,0:T(8,128)(2,1)}) %all-gather.7.cloned.1.call-update) | async-done | bytes 4587536 | tf_op jit(solution)/shard_map/all_gather | solution.py:21
  299.4 7.6 %multiply_reduce_fusion.1 = (f32[5]{0:T(128)S(1)}, f32[5,256,128]{2,1,0:T(8,128)S(1)}) fusion(bf16[5,128,3584]{2,1,0:T(8,128)(2,1)} %all-gather.7.cloned.1.call-done, f32[5,3584]{1,0:T(8,128)S(1)} %broadcast_multiply_fusion, bf16[5,256,3584]{2,1,0:T(8,128)(2,1)} %all-gather.5.cloned.1.call-done), kind=kOutput, calls=%fused_computation.18 | convolution fusion | flops 1195376640 | bytes 14489620 | tf_op jit(solution)/shard_map/lrd,lcd->lrc/dot_general | solution.py:35
  307.0 2.6 fusion.15
  309.6 0.8 reshape.34
  310.4 0.0 reduce-scatter.4.cloned.1.call-update
  310.5 39.5 %all-reduce = (f32[6]{0:T(128)S(1)}, f32[5]{0:T(128)S(1)}, f32[5,6]{1,0:T(8,128)S(1)}) all-reduce(f32[6]{0:T(128)S(1)} %get-tuple-element.11, f32[5]{0:T(128)S(1)} %get-tuple-element.13, f32[5,6]{1,0:T(8,128)S(1)} %get-tuple-element.15), channel_id=1, replica_groups=mesh['row'=4,'col'=8] {'row','col'}, use_global_device_ids=true, to_apply=%region_8.0 | all-reduce | flops 41 | bytes 328 | tf_op jit(solution)/shard_map/psum | solution.py:48
  349.9 0.7 fusion.13
  350.6 0.1 mul.53
  350.7 22.1 %reduce-scatter.4.cloned.1.call-done = f32[32,30]{1,0:T(8,128)} async-done(((f32[256,30]{1,0:T(8,128)}), f32[32,30]{1,0:T(8,128)}) %reduce-scatter.4.cloned.1.call-update) | async-done | bytes 3856
  372.8 0.8 copy.15
  373.6 0.1 broadcast_multiply_fusion.2
  373.7 0.7 copy.13
  (1 shorter events, 0.0 us)
Async XLA Ops:
  7.2 139.8 %all-gather.5.cloned.1.call-start = ((), (), s32[]{:S(2)}) async-start(), calls=%async_computation.1 | async-start | bytes 10321920 | tf_op jit(solution)/shard_map/all_gather | solution.py:17
  7.9 199.5 %all-gather.9.cloned.1.call-start = ((), (), s32[]{:S(2)}) async-start(), calls=%async_computation.4 | async-start | bytes 3538944 | tf_op jit(solution)/shard_map/all_gather | solution.py:18
  8.6 218.9 %all-gather.11.cloned.1.call-start = ((), (), s32[]{:S(2)}) async-start(), calls=%async_computation.5 | async-start | bytes 1966080 | tf_op jit(solution)/shard_map/all_gather | solution.py:22
  9.4 250.6 %all-reduce.3.cloned.1.call-start = ((), (), s32[]{:S(2)}) async-start(), calls=%async_computation.2 | async-start | bytes 229376 | tf_op jit(solution)/shard_map/psum | solution.py:24
  152.5 146.9 %all-gather.7.cloned.1.call-start = ((), (), s32[]{:S(2)}) async-start(), calls=%async_computation.3 | async-start | bytes 5734400 | tf_op jit(solution)/shard_map/all_gather | solution.py:21
  153.1 219.7 %reduce-scatter.4.cloned.1.call-start = ((), (), s32[]{:S(2)}) async-start(), calls=%async_computation.6 | async-start | bytes 147456
Sparse Core Ops, SparseCore 0:
  10.2 136.7 all-gather.4
  149.1 58.1 all-gather.8
  208.9 18.5 all-gather.10
  229.7 30.1 all-reduce.2
  261.3 38.0 all-gather.6
  310.6 62.1 reduce-scatter.3
where the time goes:
time: 382 us; the launch traced here: 381 us
  waiting for transfers between devices  291 us (76%)
  blocking collectives  50.6 us (13%)
  between operations  14.1 us (4%)
  matrix products  13.6 us (4%)
  other arithmetic  9.69 us (3%)
    all_gather x1, waiting for transfers between devices, local(): lax.all_gather(text_features, 'col', axis=1, tiled=True)  138 us
    all_gather x1, waiting for transfers between devices, local(): lax.all_gather(vision_features, 'col', axis=1, tiled=True)  54.2 us
    psum x1, blocking collectives, local(): lax.psum((cross_part, text_part, vision_part), ('row', 'col'))  39.5 us
    all_gather x1, waiting for transfers between devices, local(): lax.all_gather(text_features, 'row', axis=1, tiled=True)  38.6 us
    psum x1, waiting for transfers between devices, local(): lax.psum((jnp.sum(text_block.astype(jnp.float32), axis=1), jnp.sum(vision...  28.9 us
    unnamed x7, waiting for transfers between devices  24.8 us
    psum x1, blocking collectives, local(): lax.psum((jnp.sum(text_block.astype(jnp.float32), axis=1), jnp.sum(vision...  11.1 us
  transfers between devices with their start and end apart: 6, of which 6 were waited for; matrix products, arithmetic and copies ran while one was open for 3% of the time, Pallas kernels for 0%

commit v1 on v0

--- a/solution.py
+++ b/solution.py
@@ -18,7 +18,7 @@
         lax.all_gather(vision_features, "col", axis=1, tiled=True),
     )
     text_set, vision_set = (
-        lax.all_gather(text_features, "row", axis=1, tiled=True),
+        jnp.concatenate(lax.all_gather(text_features, "row"), axis=1),
         lax.all_gather(vision_features, "row", axis=1, tiled=True),
     )
     text_total, vision_total = lax.psum(

time: 382 us -> 386 us (1.010)
  waiting for transfers between devices: 291 us -> 282 us
  other arithmetic: 9.69 us -> 17.9 us
  local copies, waits for them, and re-layouts: 2.41 us -> 6.58 us
    all_gather x1, waiting for transfers between devices: 54.2 us -> 62.9 us  [local(): lax.all_gather(vision_features, 'col', axis=1, tiled=True)]
    convert_element_type x0 -> x2, other arithmetic: none -> 8.21 us  [the longest x1 4.65 us: center_with(): return (values - totals[:, None, :] / stimuli_count).astype(jnp.bfloat16)]
    all_gather x1, waiting for transfers between devices: 38.6 us -> 30.7 us  [local(): lax.all_gather(text_features, 'row')]
    all_gather x1, waiting for transfers between devices: 138 us -> 133 us  [local(): lax.all_gather(text_features, 'col', axis=1, tiled=True)]
    convert_element_type x0 -> x1, local copies, waits for them, and re-layouts: none -> 4.17 us  [center_with(): values = features.astype(jnp.float32)]
    psum x1, waiting for transfers between devices: 28.9 us -> 24.8 us  [local(): lax.psum((jnp.sum(text_block.astype(jnp.float32), axis=1), jnp.sum(vision...]
  transfers between devices with their start and end apart: 6 -> 6, of which waited for: 6 -> 6; matrix products, arithmetic and copies ran while one was open for 3% -> 5% of each run, Pallas kernels for 0% -> 0%
where the time goes in v1:
time: 386 us; the launch traced here: 385 us
  waiting for transfers between devices  282 us (73%)
  blocking collectives  51.9 us (13%)
  other arithmetic  17.9 us (5%)
  between operations  14.2 us (4%)
  matrix products  12.2 us (3%)
  local copies, waits for them, and re-layouts  6.58 us (2%)
    all_gather x1, waiting for transfers between devices, local(): lax.all_gather(text_features, 'col', axis=1, tiled=True)  133 us
    all_gather x1, waiting for transfers between devices, local(): lax.all_gather(vision_features, 'col', axis=1, tiled=True)  62.9 us
    psum x1, blocking collectives, local(): lax.psum((cross_part, text_part, vision_part), ('row', 'col'))  40.7 us
    all_gather x1, waiting for transfers between devices, local(): lax.all_gather(text_features, 'row')  30.7 us
    unnamed x7, waiting for transfers between devices  24.9 us
    psum x1, waiting for transfers between devices, local(): lax.psum((jnp.sum(text_block.astype(jnp.float32), axis=1), jnp.sum(vision...  24.8 us
    psum x1, blocking collectives, local(): lax.psum((jnp.sum(text_block.astype(jnp.float32), axis=1), jnp.sum(vision...  11.1 us
  transfers between devices with their start and end apart: 6, of which 6 were waited for; matrix products, arithmetic and copies ran while one was open for 5% of the time, Pallas kernels for 0%

profile of v1, /device:TPU:0, one launch (start us, length us, event | category | flops | bytes accessed | tf_op | source)
XLA Modules:
  0.0 385.5 jit_solution(2303872813381417181)
XLA Ops:
  7.2 0.7 all-gather.8.cloned.1.call-update
  7.9 0.0 all-gather.10.cloned.1.call-start
  7.9 0.7 all-gather.10.cloned.1.call-update
  8.6 0.0 all-gather.6.cloned.1.call-start
  8.7 0.7 all-gather.6.cloned.1.call-update
  9.4 0.0 all-gather.12.cloned.1.call-start
  9.4 0.5 all-gather.12.cloned.1.call-update
  10.0 0.0 all-reduce.3.cloned.1.call-start
  10.0 62.9 %all-gather.8.cloned.1.call-done = bf16[6,256,1024]{2,1,0:T(8,128)(2,1)} async-done(((bf16[6,32,1024]{2,1,0:T(8,128)(2,1)}), bf16[6,256,1024]{2,1,0:T(8,128)(2,1)}) %all-gather.8.cloned.1.call-update) | async-done | bytes 3145744 | tf_op jit(solution)/shard_map/all_gather | solution.py:18
  72.9 2.5 convert_reduce_fusion.1
  75.4 11.1 %psum.36 = f32[6,1024]{1,0:T(8,128)S(1)} all-reduce(f32[6,1024]{1,0:T(8,128)S(1)} %convert_reduce_fusion.1), channel_id=1, replica_groups=mesh['row'=4,'col'=8] {'row'}, use_global_device_ids=true, to_apply=%region_3.0 | all-reduce | flops 6144 | bytes 49152 | tf_op jit(solution)/shard_map/psum | solution.py:24
  86.6 6.5 %all-gather.10.cloned.1.call-done = bf16[6,128,1024]{2,1,0:T(8,128)(2,1)} async-done(((bf16[6,32,1024]{2,1,0:T(8,128)(2,1)}), bf16[6,128,1024]{2,1,0:T(8,128)(2,1)}) %all-gather.10.cloned.1.call-update) | async-done | bytes 1572880 | tf_op jit(solution)/shard_map/all_gather | solution.py:22
  93.1 3.4 multiply_reduce_fusion
  96.5 132.7 %all-gather.6.cloned.1.call-done = bf16[5,256,3584]{2,1,0:T(8,128)(2,1)} async-done(((bf16[5,32,3584]{2,1,0:T(8,128)(2,1)}), bf16[5,256,3584]{2,1,0:T(8,128)(2,1)}) %all-gather.6.cloned.1.call-update) | async-done | bytes 9175056 | tf_op jit(solution)/shard_map/all_gather | solution.py:17
  229.2 5.6 %convert_reduce_fusion = f32[5,3584]{1,0:T(8,128)} fusion(bf16[5,256,3584]{2,1,0:T(8,128)(2,1)} %all-gather.6.cloned.1.call-done), kind=kLoop, calls=%fused_computation.1 | loop fusion | flops 9157120 | bytes 9246720 | tf_op jit(solution)/shard_map/reduce_sum | solution.py:26
  234.8 0.0 reduce-scatter.4.cloned.1.call-start
  234.8 30.7 %all-gather.12.cloned.1.call-done = bf16[20,32,3584]{2,1,0:T(8,128)(2,1)} async-done(((bf16[5,32,3584]{2,1,0:T(8,128)(2,1)}), bf16[20,32,3584]{2,1,0:T(8,128)(2,1)}) %all-gather.12.cloned.1.call-update) | async-done | bytes 4587536 | tf_op jit(solution)/shard_map/all_gather | solution.py:21
  265.5 3.6 convert_bitcast_fusion
  269.1 4.2 %copy.12 = f32[5,4,32,3584]{3,2,1,0:T(8,128)} copy(f32[5,4,32,3584]{3,2,0,1:T(8,128)S(1)} %convert_bitcast_fusion) | data formatting | bytes 18350080 | tf_op jit(solution)/shard_map/convert_element_type | solution.py:8
  273.2 24.8 %all-reduce.3.cloned.1.call-done = f32[5,3584]{1,0:T(8,128)} async-done(((f32[5,3584]{1,0:T(8,128)}), f32[5,3584]{1,0:T(8,128)}) %all-reduce.3.cloned.1.call-update) | async-done | bytes 71696 | tf_op jit(solution)/shard_map/psum | solution.py:24
  298.1 0.9 broadcast_multiply_fusion
  299.0 4.7 %fusion.3 = bf16[5,128,3584]{2,1,0:T(8,128)(2,1)S(1)} fusion(f32[5,4,32,3584]{3,2,1,0:T(8,128)} %copy.12, f32[5,3584]{1,0:T(8,128)S(1)} %broadcast_multiply_fusion), kind=kLoop, calls=%fused_computation.6 | loop fusion | flops 4587520 | bytes 13834240 | tf_op jit(solution)/shard_map/convert_element_type | solution.py:9
  303.6 6.2 %multiply_reduce_fusion.1 = (f32[5]{0:T(128)S(1)}, f32[5,256,128]{2,1,0:T(8,128)S(1)}) fusion(bf16[5,128,3584]{2,1,0:T(8,128)(2,1)S(1)} %fusion.3, bf16[5,256,3584]{2,1,0:T(8,128)(2,1)} %all-gather.6.cloned.1.call-done, f32[5,3584]{1,0:T(8,128)S(1)} %broadcast_multiply_fusion), kind=kOutput, calls=%fused_computation.19 | convolution fusion | flops 1188495360 | bytes 14489620 | tf_op jit(solution)/shard_map/lrd,lcd->lrc/dot_general | solution.py:35
  309.9 2.6 fusion.15
  312.4 0.8 reshape.41
  313.3 40.7 %all-reduce = (f32[6]{0:T(128)S(1)}, f32[5]{0:T(128)S(1)}, f32[5,6]{1,0:T(8,128)S(1)}) all-reduce(f32[6]{0:T(128)S(1)} %get-tuple-element.11, f32[5]{0:T(128)S(1)} %get-tuple-element.13, f32[5,6]{1,0:T(8,128)S(1)} %get-tuple-element.15), channel_id=1, replica_groups=mesh['row'=4,'col'=8] {'row','col'}, use_global_device_ids=true, to_apply=%region_8.0 | all-reduce | flops 41 | bytes 328 | tf_op jit(solution)/shard_map/psum | solution.py:48
  354.0 0.7 fusion.13
  354.7 0.1 mul.53
  354.8 22.3 %reduce-scatter.4.cloned.1.call-done = f32[32,30]{1,0:T(8,128)} async-done(((f32[256,30]{1,0:T(8,128)}), f32[32,30]{1,0:T(8,128)}) %reduce-scatter.4.cloned.1.call-update) | async-done | bytes 3856
  377.1 0.8 copy.18
  377.9 0.1 broadcast_multiply_fusion.2
  377.9 0.7 copy.16
  (4 shorter events, 0.1 us)
Async XLA Ops:
  7.2 65.8 %all-gather.8.cloned.1.call-start = ((), (), s32[]{:S(2)}) async-start(), calls=%async_computation.3 | async-start | bytes 3538944 | tf_op jit(solution)/shard_map/all_gather | solution.py:18
  7.9 85.2 %all-gather.10.cloned.1.call-start = ((), (), s32[]{:S(2)}) async-start(), calls=%async_computation.4 | async-start | bytes 1966080 | tf_op jit(solution)/shard_map/all_gather | solution.py:22
  8.6 220.5 %all-gather.6.cloned.1.call-start = ((), (), s32[]{:S(2)}) async-start(), calls=%async_computation.1 | async-start | bytes 10321920 | tf_op jit(solution)/shard_map/all_gather | solution.py:17
  9.4 256.1 %all-gather.12.cloned.1.call-start = ((), (), s32[]{:S(2)}) async-start(), calls=%async_computation.5 | async-start | bytes 5734400 | tf_op jit(solution)/shard_map/all_gather | solution.py:21
  10.0 288.1 %all-reduce.3.cloned.1.call-start = ((), (), s32[]{:S(2)}) async-start(), calls=%async_computation.2 | async-start | bytes 229376 | tf_op jit(solution)/shard_map/psum | solution.py:24
  234.8 142.3 %reduce-scatter.4.cloned.1.call-start = ((), (), s32[]{:S(2)}) async-start(), calls=%async_computation.6 | async-start | bytes 147456
Sparse Core Ops, SparseCore 0:
  10.2 62.7 all-gather.7
  74.5 18.5 all-gather.9
  95.3 133.8 all-gather.5
  230.6 34.8 all-gather.11
  267.7 30.3 all-reduce.2
  313.4 63.5 reduce-scatter.3
